TPU v7x, 32 devices: a whole 2x2x4 slice. The times are simulated.
32 devices in a mesh: lat: 8 (over z, core), wave: 4 (over y, x).
Axes of the slice: x: 2, y: 2, z: 4, core: 2. Of those that a mesh axis runs over, the one named last changes fastest.
Arguments:
- spectra: bfloat16 [3, 2, 2, 768, 768], P(None, None, None, 'wave', 'lat'), may hold values from -0.01171875 to 0.01171875
- legendre: bfloat16 [16, 768, 768], P('lat', 'wave'), may hold values from -4 to 4
- wave_m: int32 [768], replicated, may hold values from 0 to 767, each once
- nlon: int32 [16], P('lat'), may hold values from 20 to 3088, as said below
- coriolis: float32 [16], P('lat'), may hold values from -1.5 to 1.5
- gauss_quadrature_weight: float32 [16], P('lat'), may hold values from 0.5 to 5
Outputs:
- tendency: float32 [2, 2, 2, 768, 768], P(None, None, None, 'wave', 'lat')
Inputs may be any that keep to these rules, and one draw needn't show every extreme that they name: `nlon`: each value is 20 + 4 i for a whole number i, and some latitude has 3088. `wave_m`: every wavenumber 0 to 767 stands in exactly one slot.
All inputs are finite; a program needn't handle non-finite values.
Results may differ from a plain program's by a relative error of at most 0.0065.
Values may be sent and summed in bfloat16 or wider, within the bound.
No kernel may reach another device: no remote copies, remote signals or barrier semaphores. Data moves between devices by JAX's collectives and lax.ppermute only.
A program may use at most 64 MiB of HBM per device.

v0:
```python
import functools
import math

import jax
import jax.numpy as jnp
from jax import lax
from jax.experimental import pallas as pl
from jax.experimental.pallas import tpu as pltpu
from jax.sharding import PartitionSpec as P

NLON = 3088
BASE = 16
LANES = 128
ORDER = {2: (1,), 4: (2, 3, 1), 8: (6, 7, 4, 5, 2, 3, 1)}
GROUPS = {2: ((0,), (1,)), 4: ((0, 1), (2, 3)), 8: ((0, 1, 2, 3), (6, 7), (4, 5))}

F32 = jnp.float32
BF16 = jnp.bfloat16

VMEM = pl.BlockSpec(memory_space=pltpu.VMEM)
SMEM = pl.BlockSpec(memory_space=pltpu.SMEM)
HBM = pl.BlockSpec(memory_space=pltpu.HBM)


def call(
    body, out_shape, in_specs, scratch=(), out_specs=VMEM, flops=0, bytes_accessed=0,
    grant=16 * 1024 * 1024,
):
    return pl.pallas_call(
        body,
        out_shape=out_shape,
        in_specs=in_specs,
        out_specs=out_specs,
        scratch_shapes=scratch,
        cost_estimate=pl.CostEstimate(
            flops=flops, bytes_accessed=bytes_accessed, transcendentals=0
        ),
        compiler_params=pltpu.CompilerParams(vmem_limit_bytes=grant),
    )


def pieces(extent, size):
    return [(first, min(first + size, extent)) for first in range(0, extent, size)]


def message_shape(rows, slots):
    if slots > LANES and slots % LANES == LANES // 2 and rows % 2 == 0:
        lines = rows * (slots // LANES) + rows // 2
        return (-(-lines // 2), 2, LANES)
    return (rows, slots)


def put_message(ref, index, value):
    if len(ref.shape) == len(index) + 2:
        ref[index] = value.astype(BF16)
        return
    rows, slots = value.shape
    lines = [value[:, first : first + LANES] for first in range(0, slots - LANES + 1, LANES)]
    rest = value[:, slots - LANES // 2 :]
    lines.append(jnp.concatenate([rest[: rows // 2], rest[rows // 2 :]], axis=1))
    if lines[-1].shape[0] % 2:
        lines.append(lines[-1][:1])
    lines = jnp.concatenate(lines, axis=0)
    for k in range(lines.shape[0] // 2):
        ref[index + (k,)] = lines[2 * k : 2 * k + 2].astype(BF16)


def get_message(message, rows, slots):
    if message.ndim == 2:
        return message
    lines = jnp.concatenate([message[k] for k in range(message.shape[0])], axis=0)
    whole = slots // LANES
    parts = [lines[k * rows : (k + 1) * rows] for k in range(whole)]
    rest = lines[whole * rows : whole * rows + rows // 2]
    half = LANES // 2
    parts.append(jnp.concatenate([rest[:, :half], rest[:, half:]], axis=0))
    return jnp.concatenate(parts, axis=1)


def turn_kernel(rank_ref, legendre_ref, *refs):
    *out_refs, turned_ref = refs
    for first, last in pieces(legendre_ref.shape[1], LANES):
        turned_ref[first:last, :] = legendre_ref[:, first:last].T
    degrees = turned_ref.shape[0] // len(out_refs)
    for d, out_ref in enumerate(out_refs):
        start = (rank_ref[0] ^ d) * degrees
        if degrees % 16 == 0:
            start = pl.multiple_of(start, 16)
        out_ref[...] = turned_ref[pl.ds(start, degrees), :]


def turn_all_kernel(legendre_ref, out_ref):
    for first, last in pieces(legendre_ref.shape[1], LANES):
        out_ref[first:last, :] = legendre_ref[:, first:last].T


def turn_spectra_kernel(repeats, fields, rank_ref, spectra_ref, ids_ref, out_ref):
    count, slots, degrees = spectra_ref.shape
    levels = count // (2 * fields)
    degree = rank_ref[0] * degrees + lax.broadcasted_iota(jnp.int32, (degrees, slots), 0)
    alive = degree >= ids_ref[...]
    for i in range(count):
        field, level, part = i // (2 * levels), (i // 2) % levels, i % 2
        turned = jnp.where(alive, spectra_ref[i].astype(F32).T, 0.0)
        place = (level * fields + field) * 2 + part
        out_ref[place] = jnp.concatenate([turned] * repeats, axis=1)


def forward_sums(legendre_refs, spectra_ref):
    degrees, columns = legendre_refs[0].shape
    fields = spectra_ref.shape[0]
    tiles = [[] for _ in legendre_refs]
    for left, right in pieces(columns, LANES):
        sums = [[None] * fields for _ in legendre_refs]
        for first, last in pieces(degrees, 16):
            own = [ref[first:last, left:right].astype(F32) for ref in legendre_refs]
            for i in range(fields):
                other = spectra_ref[i, first:last, left:right]
                for k, value in enumerate(own):
                    product = value * other
                    if last - first == 16:
                        product = product[:8] + product[8:]
                    else:
                        product = jnp.sum(product, axis=0, keepdims=True)
                    sums[k][i] = product if sums[k][i] is None else sums[k][i] + product
        for tile, values in zip(tiles, sums):
            rows = [jnp.sum(value, axis=0, keepdims=True) for value in values]
            tile.append(jnp.concatenate(rows, axis=0))
    return [jnp.concatenate(tile, axis=1) for tile in tiles]


def early_forward_kernel(spectra_ref, *refs):
    *legendre_refs, out_ref = refs
    for first, last in pieces(len(legendre_refs), 2):
        for k, value in enumerate(forward_sums(legendre_refs[first:last], spectra_ref)):
            out_ref[first + k] = value


def put_row_messages(levels, owned, slots, out_ref, a, value):
    per_level = value.shape[0] // levels
    rows = value.shape[1] // slots * levels
    for row in range(rows):
        lat, level = row // levels, row % levels
        message = value[
            level * per_level : (level + 1) * per_level, lat * slots : (lat + 1) * slots
        ]
        put_message(out_ref, (a * (rows // owned) + row // owned, row % owned), message)


def last_forward_kernel(levels, owned, slots, groups, rank_ref, spectra_ref, *refs):
    *early_refs, out_ref = refs[: len(groups) - 1] + refs[-1:]
    legendre_refs = refs[len(groups) - 1 : -1]
    put = functools.partial(put_row_messages, levels, owned, slots, out_ref)
    for places, ref in zip(groups[:-1], early_refs):
        for k, d in enumerate(places):
            put(rank_ref[0] ^ d, ref[k])
    for first, last in pieces(len(legendre_refs), 2):
        values = forward_sums(legendre_refs[first:last], spectra_ref)
        for d, value in zip(groups[-1][first:last], values):
            put(rank_ref[0] ^ d, value)


def loop_forward_kernel(levels, owned, slots, spectra_ref, legendre_ref, out_ref):
    def one_source(a, carry):
        (value,) = forward_sums([legendre_ref.at[a]], spectra_ref)
        put_row_messages(levels, owned, slots, out_ref, a, value)
        return carry

    lax.fori_loop(0, legendre_ref.shape[0], one_source, 0)


def cos_sin(places, ids, count, inverse):
    quads = 4.0 * places * ids
    turns = jnp.floor(quads * inverse + 0.5)
    angle = (quads - turns * count) * (inverse * (math.pi / 2))
    square = angle * angle
    c = 1.0 + square * (-1 / 2 + square * (1 / 24 + square * (-1 / 720 + square * (1 / 40320))))
    s = angle * (
        1.0 + square * (-1 / 6 + square * (1 / 120 + square * (-1 / 5040 + square * (1 / 362880))))
    )
    quadrant = turns - 4.0 * jnp.floor(turns * 0.25)
    odd = (quadrant == 1.0) | (quadrant == 3.0)
    cosine = jnp.where(odd, s, c)
    sine = jnp.where(odd, c, s)
    cosine = jnp.where((quadrant == 1.0) | (quadrant == 2.0), -cosine, cosine)
    sine = jnp.where(quadrant >= 2.0, -sine, sine)
    return cosine, sine


def image_signs(ids):
    quadrant = ids - 4.0 * jnp.floor(ids * 0.25)
    one = jnp.ones_like(ids)
    none = jnp.zeros_like(ids)
    parity = jnp.where((quadrant == 1.0) | (quadrant == 3.0), -1.0, 1.0)
    c = jnp.where(quadrant == 0.0, 1.0, jnp.where(quadrant == 2.0, -1.0, 0.0))
    s = jnp.where(quadrant == 1.0, 1.0, jnp.where(quadrant == 3.0, -1.0, 0.0))
    cos_cos = [one, one, parity, parity, c, c, c, c]
    cos_sin = [none, none, none, none, s, -s, -s, s]
    sin_cos = [none, none, none, none, s, s, -s, -s]
    sin_sin = [one, -one, -parity, parity, -c, c, -c, c]
    return [jnp.concatenate(rows, axis=0) for rows in (cos_cos, cos_sin, sin_cos, sin_sin)]


def table_kernel(
    levels, rank_ref, nlon_ref, coriolis_ref, weight_ref, ids_ref,
    table_ref, left_ref, right_ref, share_ref, rotation_ref, base_ref, step_ref,
):
    owned = table_ref.shape[0]
    steps = step_ref.shape[1]
    waves = ids_ref.shape[1]
    ids = ids_ref[...].astype(F32)
    signs = image_signs(ids)
    for offset in range(owned):
        latitude = (rank_ref[0] * owned + offset) // levels
        count_int = nlon_ref[latitude]
        count = jnp.full((1, waves), count_int.astype(F32))
        inverse = 1.0 / count
        rows = lax.broadcasted_iota(jnp.int32, (BASE, waves), 0).astype(F32)
        base_ref[0], base_ref[1] = cos_sin(rows, ids, count, inverse)
        rows = lax.broadcasted_iota(jnp.int32, (steps, waves), 0).astype(F32) * BASE
        step_ref[0], step_ref[1] = cos_sin(rows, ids, count, inverse)
        for a in range(steps):
            step_c = step_ref[0, a : a + 1, :]
            step_s = step_ref[1, a : a + 1, :]
            base_c = base_ref[0]
            base_s = base_ref[1]
            here = slice(a * BASE, (a + 1) * BASE)
            table_ref[offset, here, :waves] = (step_c * base_c - step_s * base_s).astype(BF16)
            table_ref[offset, here, waves:] = (step_s * base_c + step_c * base_s).astype(BF16)

        factor = jnp.where(ids == 0.0, 1.0, 2.0)
        factor = jnp.where(2.0 * ids < count, factor, 0.0)
        scale = jnp.where(factor > 0.0, weight_ref[latitude] / count, 0.0)
        left_ref[offset, 0] = signs[0] * factor
        left_ref[offset, 1] = -signs[2] * factor
        left_ref[offset, 2] = signs[1] * factor
        left_ref[offset, 3] = -signs[3] * factor
        right_ref[offset, 0] = signs[0] * scale
        right_ref[offset, 1] = signs[1] * scale
        right_ref[offset, 2] = -signs[2] * scale
        right_ref[offset, 3] = -signs[3] * scale
        place = lax.broadcasted_iota(jnp.int32, share_ref.shape[1:], 1)
        share = jnp.where((place == 0) | (8 * place == count_int), 0.5, 1.0)
        share_ref[offset] = jnp.where(8 * place <= count_int, share, 0.0)
        rotation_ref[offset] = jnp.full(rotation_ref.shape[1:], coriolis_ref[latitude])


def grid_kernel(
    slots, partial_ref, table_ref, left_ref, right_ref, share_ref, rotation_ref, out_ref, rows_ref
):
    owned = partial_ref.shape[1]
    waves = left_ref.shape[-1]
    parts = waves // slots
    sources = partial_ref.shape[0] // parts
    for offset in range(owned):

        def total(w):
            def add(a, value):
                return value + partial_ref[a * parts + w, offset].astype(F32)

            if sources > 8:
                return lax.fori_loop(1, sources, add, partial_ref[w, offset].astype(F32))
            value = partial_ref[w, offset].astype(F32)
            for a in range(1, sources):
                value = add(a, value)
            return value

        fourier = jnp.concatenate(
            [get_message(total(w), 6, slots) for w in range(parts)], axis=1
        )
        fourier = fourier.astype(BF16).astype(F32)
        for field in range(3):
            here = slice(8 * field, 8 * field + 8)
            real = fourier[2 * field : 2 * field + 1]
            imag = fourier[2 * field + 1 : 2 * field + 2]
            rows_ref[here, :waves] = real * left_ref[offset, 0] + imag * left_ref[offset, 1]
            rows_ref[here, waves:] = real * left_ref[offset, 2] + imag * left_ref[offset, 3]
        grid = lax.dot_general(
            rows_ref[...].astype(BF16),
            table_ref[offset],
            (((1,), (1,)), ((), ())),
            preferred_element_type=F32,
        )
        vorticity, divergence, temperature = grid[0:8], grid[8:16], grid[16:24]
        share = share_ref[offset]

        def shared(product):
            rounded = jnp.where(share > 0.0, product, 0.0).astype(BF16)
            return rounded.astype(F32) * share

        stretch = shared(-(vorticity + rotation_ref[offset]) * divergence)
        heating = shared(-temperature * divergence)
        products = jnp.concatenate([stretch, heating], axis=0).astype(BF16)
        sums = jnp.dot(products, table_ref[offset], preferred_element_type=F32)
        both = []
        for q in range(2):
            c = sums[8 * q : 8 * q + 8, :waves]
            s = sums[8 * q : 8 * q + 8, waves:]
            for k in range(2):
                term = c * right_ref[offset, 2 * k] + s * right_ref[offset, 2 * k + 1]
                both.append(jnp.sum(term, axis=0, keepdims=True))
        back = jnp.concatenate(both, axis=0)
        for w in range(parts):
            part = back[:, w * slots : (w + 1) * slots]

            def put(a, carry):
                put_message(out_ref, (a * parts + w, offset), part)
                return carry

            if sources > 8:
                lax.fori_loop(0, sources, put, 0)
            else:
                for a in range(sources):
                    put(a, 0)


def backward_kernel(levels, rank_ref, back_ref, ids_ref, *refs):
    *legendre_refs, out_ref, wide_ref, sums_ref, done_ref, sems = refs
    sources, _, _, columns = wide_ref.shape
    degrees = sums_ref.shape[1]
    outs, slots, _ = out_ref.shape
    lats = columns // slots
    owned = back_ref.shape[1]
    targets = back_ref.shape[0] // sources
    apart = len(legendre_refs) > 1

    def spread(k, a):
        for level in range(levels):
            rows = []
            for lat in range(lats):
                row = lat * levels + level
                rows.append(back_ref[a * targets + row // owned, row % owned].astype(F32))
            both = jnp.concatenate(rows, axis=1)
            for i in range(4):
                place = ((i // 2) * levels + level) * 2 + i % 2
                wide_ref[k, place] = jnp.broadcast_to(both[i : i + 1], (8, columns))

    if apart:
        for d in range(sources):
            spread(d, rank_ref[0] ^ d)
    else:
        lax.fori_loop(0, sources, lambda a, carry: spread(a, a) or carry, 0)

    degree = rank_ref[0] * degrees + lax.broadcasted_iota(jnp.int32, (degrees, slots), 0)
    alive = degree >= ids_ref[...]
    copies = []
    for own in pieces(outs, outs):
        for first, last in pieces(degrees, 16):
            for left, right in pieces(columns, LANES):

                def add(k, piece, sums):
                    piece = piece.astype(F32)
                    added = []
                    for i in range(*own):
                        other = wide_ref[k, i, :, left:right]
                        other = jnp.concatenate([other, other], axis=0)[: last - first]
                        term = piece * other
                        past = sums[i - own[0]]
                        added.append(term if past is None else past + term)
                    return tuple(added)

                count = own[1] - own[0]
                if apart:
                    sums = (None,) * count
                    for k, ref in enumerate(legendre_refs):
                        sums = add(k, ref[first:last, left:right], sums)
                else:
                    sums = lax.fori_loop(
                        0,
                        sources,
                        lambda a, sums: add(a, legendre_refs[0][a, first:last, left:right], sums),
                        (jnp.zeros((last - first, right - left), F32),) * count,
                    )
                for i in range(*own):
                    sums_ref[i, first:last, left:right] = sums[i - own[0]]
        for i in range(*own):
            value = sums_ref[i]
            folded = value[:, :slots]
            for lat in range(1, lats):
                folded = folded + value[:, lat * slots : (lat + 1) * slots]
            done_ref[i] = jnp.where(alive, folded, 0.0).T
            copies.append(pltpu.make_async_copy(done_ref.at[i], out_ref.at[i], sems.at[i]))
            copies[-1].start()
    for copy in copies:
        copy.wait()


def local(n_lat, n_wave, spectra, legendre, wave_m, nlon, coriolis, gauss_quadrature_weight):
    lats, slots, total = legendre.shape
    fields, levels = spectra.shape[:2]
    waves = wave_m.shape[0]
    degrees = spectra.shape[4]
    columns = lats * slots
    owned = lats * levels // n_wave
    lat_rank = lax.axis_index("lat").reshape(1)
    wave_rank = lax.axis_index("wave").reshape(1)
    steps = -(-(NLON // 8 + 1) // BASE)
    places = steps * BASE

    rows = legendre.reshape(columns, total)
    apart = n_lat in (2, 4, 8)
    if apart:
        blocks = call(
            turn_kernel,
            (jax.ShapeDtypeStruct((degrees, columns), BF16),) * n_lat,
            [SMEM, VMEM],
            [pltpu.VMEM((total, columns), BF16)],
            out_specs=(VMEM,) * n_lat,
            bytes_accessed=4 * total * columns,
        )(lat_rank, rows)
        turned = {0: blocks[0]}
        for d in ORDER[n_lat]:
            turned[d] = lax.ppermute(blocks[d], "lat", [(i, i ^ d) for i in range(n_lat)])
    else:
        blocks = call(
            turn_all_kernel,
            jax.ShapeDtypeStruct((total, columns), BF16),
            [VMEM],
            bytes_accessed=4 * total * columns,
        )(rows)
        blocks = lax.all_to_all(blocks.reshape(n_lat, degrees, columns), "lat", 0, 0, tiled=True)
        turned = {0: blocks}

    own_ids = lax.dynamic_slice_in_dim(wave_m, wave_rank[0] * slots, slots, 0).reshape(1, slots)
    all_ids = wave_m.reshape(1, waves)
    spectra_turned = call(
        functools.partial(turn_spectra_kernel, lats, fields),
        jax.ShapeDtypeStruct((2 * fields * levels, degrees, columns), F32),
        [SMEM, VMEM, VMEM],
        flops=10 * fields * levels * degrees * columns,
        bytes_accessed=8 * fields * levels * degrees * columns,
    )(lat_rank, spectra.reshape(2 * fields * levels, slots, degrees), own_ids)

    row = call(
        functools.partial(table_kernel, levels),
        (
            jax.ShapeDtypeStruct((owned, places, 2 * waves), BF16),
            jax.ShapeDtypeStruct((owned, 4, 8, waves), F32),
            jax.ShapeDtypeStruct((owned, 4, 8, waves), F32),
            jax.ShapeDtypeStruct((owned, 8, places), F32),
            jax.ShapeDtypeStruct((owned, 8, places), F32),
        ),
        [SMEM, SMEM, SMEM, SMEM, VMEM],
        [pltpu.VMEM((2, BASE, waves), F32), pltpu.VMEM((2, steps, waves), F32)],
        out_specs=(VMEM,) * 5,
        flops=16 * owned * places * waves,
        bytes_accessed=4 * owned * places * waves,
    )(wave_rank, nlon, coriolis, gauss_quadrature_weight, all_ids)
    spectra_turned, *row = lax.optimization_barrier((spectra_turned, *row))

    message = jax.ShapeDtypeStruct(
        (n_lat * n_wave, owned) + message_shape(2 * fields, slots), BF16
    )
    cost = 4 * fields * levels * degrees * columns
    if apart:
        groups = GROUPS[n_lat]
        early = []
        for part in groups[:-1]:
            early.append(
                call(
                    early_forward_kernel,
                    jax.ShapeDtypeStruct((len(part), 2 * fields * levels, columns), F32),
                    [VMEM] * (1 + len(part)),
                    flops=len(part) * cost,
                    bytes_accessed=cost,
                )(spectra_turned, *[turned[d] for d in part])
            )
        partial = call(
            functools.partial(last_forward_kernel, levels, owned, slots, groups),
            message,
            [SMEM] + [VMEM] * (len(groups) + len(groups[-1])),
            flops=len(groups[-1]) * cost,
            bytes_accessed=cost,
        )(lat_rank, spectra_turned, *early, *[turned[d] for d in groups[-1]])
    else:
        partial = call(
            functools.partial(loop_forward_kernel, levels, owned, slots),
            message,
            [VMEM, VMEM],
            flops=n_lat * cost,
            bytes_accessed=cost,
        )(spectra_turned, turned[0])
    partial = lax.all_to_all(partial, ("lat", "wave"), 0, 0, tiled=True)

    back = call(
        functools.partial(grid_kernel, slots),
        jax.ShapeDtypeStruct((n_lat * n_wave, owned, 4, slots), BF16),
        [VMEM] * 6,
        [pltpu.VMEM((24, 2 * waves), F32)],
        flops=128 * owned * places * waves,
        bytes_accessed=4 * owned * places * waves,
    )(partial, *row)
    back = lax.all_to_all(back, ("lat", "wave"), 0, 0, tiled=True)

    outs = 4 * levels
    out = call(
        functools.partial(backward_kernel, levels),
        jax.ShapeDtypeStruct((outs, slots, degrees), F32),
        [SMEM, VMEM, VMEM] + [VMEM] * len(turned),
        [
            pltpu.VMEM((n_lat, outs, 8, columns), F32),
            pltpu.VMEM((outs, degrees, columns), F32),
            pltpu.VMEM((outs, slots, degrees), F32),
            pltpu.SemaphoreType.DMA((outs,)),
        ],
        out_specs=HBM,
        flops=2 * n_lat * outs * degrees * columns,
        bytes_accessed=8 * outs * degrees * slots,
    )(lat_rank, back, own_ids, *[turned[d] for d in sorted(turned)])
    return out.reshape(2, levels, 2, slots, degrees)


def solution(mesh):
    placed = (
        P(None, None, None, "wave", "lat"),
        P("lat", "wave", None),
        P(),
        P("lat"),
        P("lat"),
        P("lat"),
    )
    n_lat = mesh.shape["lat"]
    return jax.shard_map(
        functools.partial(local, n_lat, mesh.shape["wave"]),
        mesh=mesh,
        in_specs=placed,
        out_specs=P(None, None, None, "wave", "lat"),
        check_vma=False,
    )
```

profile of v0, /device:TPU:0, one launch (start us, length us, event | category | flops | bytes accessed | tf_op | source)
XLA Modules:
  0.0 44.0 jit_solution(14895856780652626318)
XLA Ops:
  0.0 0.0 copy-start.4
  0.0 0.0 copy-start.3
  0.0 0.0 copy-start.2
  0.0 0.0 copy-start
  0.0 1.1 %copy-done = bf16[2,192,768]{2,1,0:T(8,128)(2,1)S(1)} copy-done((bf16[2,192,768]{2,1,0:T(8,128)(2,1)S(1)}, bf16[2,192,768]{2,1,0:T(8,128)(2,1)}, u32[]{:S(2)}) %copy-start) | copy-done | bytes 589848
  1.1 0.3 shard_map.66
  1.4 5.1 %collective-permute-start.3 = (bf16[96,384]{1,0:T(8,128)(2,1)S(1)}, bf16[96,384]{1,0:T(8,128)(2,1)S(1)}, u32[]{:S(2)}, u32[]{:S(2)}) collective-permute-start(bf16[96,384]{1,0:T(8,128)(2,1)S(1)} %get-tuple-element.34), channel_id=1, source_target_pairs={{0,24},{4,28},{8,16},{12,20},{16,8},{20,12},{24,0},{28,4},{1,25},{... | collective-permute-start | bytes 221192 | tf_op jit(solution)/shard_map/ppermute | solution.py:413
  6.5 0.0 collective-permute-start.4
  6.5 0.2 collective-permute-start
  6.7 0.0 collective-permute-start.1
  6.7 1.7 %collective-permute-start.2 = (bf16[96,384]{1,0:T(8,128)(2,1)S(1)}, bf16[96,384]{1,0:T(8,128)(2,1)S(1)}, u32[]{:S(2)}, u32[]{:S(2)}) collective-permute-start(bf16[96,384]{1,0:T(8,128)(2,1)S(1)} %get-tuple-element.33), channel_id=1, source_target_pairs={{0,12},{4,8},{8,4},{12,0},{16,28},{20,24},{24,20},{28,16},{1,13},{... | collective-permute-start | bytes 221192 | tf_op jit(solution)/shard_map/ppermute | solution.py:413
  8.4 0.8 %collective-permute-done.3.refs_0_.refs_6_ = bf16[96,384]{1,0:T(8,128)(2,1)S(1)} collective-permute-done((bf16[96,384]{1,0:T(8,128)(2,1)S(1)}, bf16[96,384]{1,0:T(8,128)(2,1)S(1)}, u32[]{:S(2)}, u32[]{:S(2)}) %collective-permute-start.3) | collective-permute-done | bytes 73760 | tf_op jit(solution)/shard_map/ppermute | solution.py:413
  9.2 4.0 %collective-permute-start.5 = (bf16[96,384]{1,0:T(8,128)(2,1)S(1)}, bf16[96,384]{1,0:T(8,128)(2,1)S(1)}, u32[]{:S(2)}, u32[]{:S(2)}) collective-permute-start(bf16[96,384]{1,0:T(8,128)(2,1)S(1)} %get-tuple-element.36), channel_id=1, source_target_pairs={{0,16},{4,20},{8,24},{12,28},{16,0},{20,4},{24,8},{28,12},{1,17},{... | collective-permute-start | bytes 221192 | tf_op jit(solution)/shard_map/ppermute | solution.py:413
  13.2 0.0 collective-permute-done.4.refs_1_.refs_7_
  13.2 1.0 %collective-permute-start.6 = (bf16[96,384]{1,0:T(8,128)(2,1)S(1)}, bf16[96,384]{1,0:T(8,128)(2,1)S(1)}, u32[]{:S(2)}, u32[]{:S(2)}) collective-permute-start(bf16[96,384]{1,0:T(8,128)(2,1)S(1)} %get-tuple-element.37), channel_id=1, source_target_pairs={{0,20},{4,16},{8,28},{12,24},{16,4},{20,0},{24,12},{28,8},{1,21},{... | collective-permute-start | bytes 221192 | tf_op jit(solution)/shard_map/ppermute | solution.py:413
  14.2 0.7 %reshape.25.ids_ref = s32[1,768]{1,0:T(1,128)S(1)} reshape(s32[768]{0:T(1024)} %param.8) | data formatting | bytes 6144 | tf_op jit(solution)/shard_map/reshape | solution.py:425
  14.9 0.8 %dynamic_slice.3 = s32[192]{0:T(256)S(1)} dynamic-slice(s32[768]{0:T(1024)} %param.8, s32[]{:T(128)S(6)} %select_n.3), dynamic_slice_sizes={192} | dynamic-slice | bytes 1540 | tf_op jit(solution)/shard_map/dynamic_slice | solution.py:424
  15.6 0.0 copy-start.1
  15.6 1.1 %copy-done.1 = bf16[3,2,2,192,96]{4,3,2,1,0:T(8,128)(2,1)S(1)} copy-done((bf16[3,2,2,192,96]{4,3,2,1,0:T(8,128)(2,1)S(1)}, bf16[3,2,2,192,96]{4,3,2,1,0:T(8,128)(2,1)}, u32[]{:S(2)}) %copy-start.1) | copy-done | bytes 442392
  16.7 0.4 shard_map.64.spectra_ref
  17.1 0.0 copy-done.4
  17.1 0.0 copy-done.3
  17.2 0.0 copy-done.2
  17.2 1.2 %shard_map.65 = (bf16[1,400,1536]{2,1,0:T(8,128)(2,1)S(1)}, f32[1,4,8,768]{3,2,1,0:T(8,128)S(1)}, f32[1,4,8,768]{3,2,1,0:T(8,128)S(1)}, f32[1,8,400]{2,1,0:T(8,128)S(1)}, f32[1,8,400]{2,1,0:T(8,128)S(1)}) custom-call(s32[1]{0:T(128)} %bitcast.3.rank_ref, s32[2]{0:T(128)S(1)} %copy-done.2, f32[2]{0:T(128)S(1)} %copy-done.3, f32[2]{0:T(128)S(1)} %copy-done.4, ...), custom_call_target="tpu_custom_call" | custom-call | flops 4915200 | bytes 1228800 | tf_op jit(solution)/shard_map/pallas_call | solution.py:434
  18.4 0.3 shard_map.68.refs_1_
  18.7 0.0 collective-permute-done.refs_1_
  18.7 0.0 collective-permute-done.1.refs_2_
  18.7 0.0 collective-permute-done.2.refs_3_
  18.7 0.6 %shard_map.67.refs_0_ = f32[4,12,384]{2,1,0:T(8,128)S(1)} custom-call(f32[12,96,384]{2,1,0:T(8,128)S(1)} %shard_map.64.spectra_ref, bf16[96,384]{1,0:T(8,128)(2,1)S(1)} %get-tuple-element.30.refs_0_, bf16[96,384]{1,0:T(8,128)(2,1)S(1)} %collective-permute-done.refs_1_, bf16[96,384]{1,0:T(8,128)(2,1)S(1)} %collective-permute-done.1.refs_2_, ...), custom_call_target="tpu_custom_call" | custom-call | flops 3538944 | bytes 884736 | tf_op jit(solution)/shard_map/pallas_call | solution.py:460
  19.3 0.0 collective-permute-done.5.refs_2_.refs_4_
  19.3 1.2 %collective-permute-done.6.refs_3_.refs_5_ = bf16[96,384]{1,0:T(8,128)(2,1)S(1)} collective-permute-done((bf16[96,384]{1,0:T(8,128)(2,1)S(1)}, bf16[96,384]{1,0:T(8,128)(2,1)S(1)}, u32[]{:S(2)}, u32[]{:S(2)}) %collective-permute-start.6) | collective-permute-done | bytes 73760 | tf_op jit(solution)/shard_map/ppermute | solution.py:413
  20.6 0.5 %shard_map.69 = bf16[32,1,5,2,128]{4,3,2,1,0:T(2,128)(2,1)S(1)} custom-call(s32[1]{0:T(128)} %bitcast.rank_ref, f32[12,96,384]{2,1,0:T(8,128)S(1)} %shard_map.64.spectra_ref, f32[4,12,384]{2,1,0:T(8,128)S(1)} %shard_map.67.refs_0_, f32[2,12,384]{2,1,0:T(8,128)S(1)} %shard_map.68.refs_1_, bf16[96,384]{1,0:T(8,128)(2,1)S(1)} %collective-permute-done.5.refs_2_.refs_4_, ...), custom_call_target="tpu_custom_call" | custom-call | flops 1769472 | bytes 884736 | tf_op jit(solution)/shard_map/pallas_call | solution.py:468
  21.1 11.0 %all_to_all.10.partial_ref = bf16[32,1,5,2,128]{4,3,2,1,0:T(2,128)(2,1)S(1)} all-to-all(bf16[32,1,5,2,128]{4,3,2,1,0:T(2,128)(2,1)S(1)} %shard_map.69), channel_id=1, replica_groups=mesh['lat'=8,'wave'=4] {'lat','wave'}, dimensions={0} | all-to-all | bytes 163840 | tf_op jit(solution)/shard_map/all_to_all | solution.py:483
  32.1 1.0 %shard_map.70 = bf16[32,1,4,192]{3,2,1,0:T(4,128)(2,1)S(1)} custom-call(bf16[32,1,5,2,128]{4,3,2,1,0:T(2,128)(2,1)S(1)} %all_to_all.10.partial_ref, bf16[1,400,1536]{2,1,0:T(8,128)(2,1)S(1)} %get-tuple-element.38.table_ref, f32[1,4,8,768]{3,2,1,0:T(8,128)S(1)} %get-tuple-element.39.left_ref, f32[1,4,8,768]{3,2,1,0:T(8,128)S(1)} %get-tuple-element.40.right_ref, ...), custom_call_target="tpu_custom_call" | custom-call | flops 39321600 | bytes 1228800 | tf_op jit(solution)/shard_map/pallas_call | solution.py:485
  33.1 9.2 %all_to_all.11.back_ref = bf16[32,1,4,192]{3,2,1,0:T(4,128)(2,1)S(1)} all-to-all(bf16[32,1,4,192]{3,2,1,0:T(4,128)(2,1)S(1)} %shard_map.70), channel_id=1, replica_groups=mesh['lat'=8,'wave'=4] {'lat','wave'}, dimensions={0} | all-to-all | bytes 98304 | tf_op jit(solution)/shard_map/all_to_all | solution.py:493
  42.3 1.7 %shard_map.71 = f32[8,192,96]{2,1,0:T(8,128)} custom-call(s32[1]{0:T(128)} %bitcast.rank_ref, bf16[32,1,4,192]{3,2,1,0:T(4,128)(2,1)S(1)} %all_to_all.11.back_ref, s32[1,192]{1,0:T(1,128)S(1)} %bitcast.9, bf16[96,384]{1,0:T(8,128)(2,1)S(1)} %get-tuple-element.30.refs_0_, bf16[96,384]{1,0:T(8,128)(2,1)S(1)} %collective-permute-done.refs_1_, ...), custom_call_target="tpu_custom_call" | custom-call | flops 4718592 | bytes 1179648 | tf_op jit(solution)/shard_map/pallas_call | solution.py:496
Async XLA Ops:
  0.0 17.1 %copy-start.4 = (f32[2]{0:T(128)S(1)}, f32[2]{0:T(128)}, u32[]{:S(2)}) copy-start(f32[2]{0:T(128)} %weight_ref.1) | copy-start | bytes 28
  0.0 17.1 %copy-start.3 = (f32[2]{0:T(128)S(1)}, f32[2]{0:T(128)}, u32[]{:S(2)}) copy-start(f32[2]{0:T(128)} %coriolis_ref.1) | copy-start | bytes 28
  0.0 17.2 %copy-start.2 = (s32[2]{0:T(128)S(1)}, s32[2]{0:T(128)}, u32[]{:S(2)}) copy-start(s32[2]{0:T(128)} %nlon_ref.1) | copy-start | bytes 28
  0.0 1.1 %copy-start = (bf16[2,192,768]{2,1,0:T(8,128)(2,1)S(1)}, bf16[2,192,768]{2,1,0:T(8,128)(2,1)}, u32[]{:S(2)}) copy-start(bf16[2,192,768]{2,1,0:T(8,128)(2,1)} %param.7) | copy-start | bytes 1769476
  1.4 7.8 %collective-permute-start.3 = (bf16[96,384]{1,0:T(8,128)(2,1)S(1)}, bf16[96,384]{1,0:T(8,128)(2,1)S(1)}, u32[]{:S(2)}, u32[]{:S(2)}) collective-permute-start(bf16[96,384]{1,0:T(8,128)(2,1)S(1)} %get-tuple-element.34), channel_id=1, source_target_pairs={{0,24},{4,28},{8,16},{12,20},{16,8},{20,12},{24,0},{28,4},{1,25},{... | collective-permute-start | bytes 221192 | tf_op jit(solution)/shard_map/ppermute | solution.py:413
  6.5 6.7 %collective-permute-start.4 = (bf16[96,384]{1,0:T(8,128)(2,1)S(1)}, bf16[96,384]{1,0:T(8,128)(2,1)S(1)}, u32[]{:S(2)}, u32[]{:S(2)}) collective-permute-start(bf16[96,384]{1,0:T(8,128)(2,1)S(1)} %get-tuple-element.35), channel_id=1, source_target_pairs={{0,28},{4,24},{8,20},{12,16},{16,12},{20,8},{24,4},{28,0},{1,29},{... | collective-permute-start | bytes 221192 | tf_op jit(solution)/shard_map/ppermute | solution.py:413
  6.5 12.2 %collective-permute-start = (bf16[96,384]{1,0:T(8,128)(2,1)S(1)}, bf16[96,384]{1,0:T(8,128)(2,1)S(1)}, u32[]{:S(2)}, u32[]{:S(2)}) collective-permute-start(bf16[96,384]{1,0:T(8,128)(2,1)S(1)} %get-tuple-element.31), channel_id=1, source_target_pairs={{0,4},{4,0},{8,12},{12,8},{16,20},{20,16},{24,28},{28,24},{1,5},{5... | collective-permute-start | bytes 221192 | tf_op jit(solution)/shard_map/ppermute | solution.py:413
  6.7 12.0 %collective-permute-start.1 = (bf16[96,384]{1,0:T(8,128)(2,1)S(1)}, bf16[96,384]{1,0:T(8,128)(2,1)S(1)}, u32[]{:S(2)}, u32[]{:S(2)}) collective-permute-start(bf16[96,384]{1,0:T(8,128)(2,1)S(1)} %get-tuple-element.32), channel_id=1, source_target_pairs={{0,8},{4,12},{8,0},{12,4},{16,24},{20,28},{24,16},{28,20},{1,9},{5... | collective-permute-start | bytes 221192 | tf_op jit(solution)/shard_map/ppermute | solution.py:413
  6.7 12.0 %collective-permute-start.2 = (bf16[96,384]{1,0:T(8,128)(2,1)S(1)}, bf16[96,384]{1,0:T(8,128)(2,1)S(1)}, u32[]{:S(2)}, u32[]{:S(2)}) collective-permute-start(bf16[96,384]{1,0:T(8,128)(2,1)S(1)} %get-tuple-element.33), channel_id=1, source_target_pairs={{0,12},{4,8},{8,4},{12,0},{16,28},{20,24},{24,20},{28,16},{1,13},{... | collective-permute-start | bytes 221192 | tf_op jit(solution)/shard_map/ppermute | solution.py:413
  9.2 10.1 %collective-permute-start.5 = (bf16[96,384]{1,0:T(8,128)(2,1)S(1)}, bf16[96,384]{1,0:T(8,128)(2,1)S(1)}, u32[]{:S(2)}, u32[]{:S(2)}) collective-permute-start(bf16[96,384]{1,0:T(8,128)(2,1)S(1)} %get-tuple-element.36), channel_id=1, source_target_pairs={{0,16},{4,20},{8,24},{12,28},{16,0},{20,4},{24,8},{28,12},{1,17},{... | collective-permute-start | bytes 221192 | tf_op jit(solution)/shard_map/ppermute | solution.py:413
  13.2 7.3 %collective-permute-start.6 = (bf16[96,384]{1,0:T(8,128)(2,1)S(1)}, bf16[96,384]{1,0:T(8,128)(2,1)S(1)}, u32[]{:S(2)}, u32[]{:S(2)}) collective-permute-start(bf16[96,384]{1,0:T(8,128)(2,1)S(1)} %get-tuple-element.37), channel_id=1, source_target_pairs={{0,20},{4,16},{8,28},{12,24},{16,4},{20,0},{24,12},{28,8},{1,21},{... | collective-permute-start | bytes 221192 | tf_op jit(solution)/shard_map/ppermute | solution.py:413
  15.6 1.1 %copy-start.1 = (bf16[3,2,2,192,96]{4,3,2,1,0:T(8,128)(2,1)S(1)}, bf16[3,2,2,192,96]{4,3,2,1,0:T(8,128)(2,1)}, u32[]{:S(2)}) copy-start(bf16[3,2,2,192,96]{4,3,2,1,0:T(8,128)(2,1)} %param.6) | copy-start | bytes 1327108
where the time goes:
time: 44.2 us; the launch traced here: 44 us
  blocking collectives  20.2 us (46%)
  starting transfers between devices  12 us (27%)
  Pallas kernels  6 us (14%)
  local copies, waits for them, and re-layouts  3.63 us (8%)
  waiting for transfers between devices  2.04 us (5%)
    ppermute x7, starting transfers between devices, local(): lax.ppermute(blocks[d], 'lat', [(i, i ^ d) for i in range(n_lat)])  12 us
    all_to_all x1, blocking collectives, local(): partial = lax.all_to_all(partial, ('lat', 'wave'), 0, 0, tiled=True)  11 us
    all_to_all x1, blocking collectives, local(): back = lax.all_to_all(back, ('lat', 'wave'), 0, 0, tiled=True)  9.18 us
    unnamed x10, local copies, waits for them, and re-layouts  2.18 us
    ppermute x7, waiting for transfers between devices, local(): lax.ppermute(blocks[d], 'lat', [(i, i ^ d) for i in range(n_lat)])  2.04 us
    pallas_call x1, Pallas kernels, local(): call(functools.partial(backward_kernel, levels), jax.ShapeDtypeStruct((ou...  1.69 us
    pallas_call x1, Pallas kernels, local(): call(functools.partial(table_kernel, levels), (jax.ShapeDtypeStruct((owne...  1.19 us
    pallas_call x1, Pallas kernels, local(): call(functools.partial(grid_kernel, slots), jax.ShapeDtypeStruct((n_lat *...  1 us
  transfers between devices with their start and end apart: 7, of which 2 were waited for; matrix products, arithmetic and copies ran while one was open for 3% of the time, Pallas kernels for 6%

commit v1 on v0

--- a/solution.py
+++ b/solution.py
@@ -11,8 +11,9 @@
 NLON = 3088
 BASE = 16
 LANES = 128
-ORDER = {2: (1,), 4: (2, 3, 1), 8: (6, 7, 4, 5, 2, 3, 1)}
-GROUPS = {2: ((0,), (1,)), 4: ((0, 1), (2, 3)), 8: ((0, 1, 2, 3), (6, 7), (4, 5))}
+WORK = 128
+ORDER = {2: (1,), 4: (2, 3, 1), 8: (6, 4, 7, 5, 2, 3, 1)}
+GROUPS = {2: ((0,), (1,)), 4: ((0, 1), (2, 3)), 8: ((0, 1, 2, 3), (6, 7), (4,), (5,))}
 
 F32 = jnp.float32
 BF16 = jnp.bfloat16
@@ -39,6 +40,10 @@
     )
 
 
+def far(value):
+    return pltpu.with_memory_space_constraint(value, pltpu.HBM)
+
+
 def pieces(extent, size):
     return [(first, min(first + size, extent)) for first in range(0, extent, size)]
 
@@ -94,14 +99,20 @@
         out_ref[first:last, :] = legendre_ref[:, first:last].T
 
 
-def turn_spectra_kernel(repeats, fields, rank_ref, spectra_ref, ids_ref, out_ref):
+def turn_spectra_kernel(
+    repeats, fields, lat_ref, wave_ref, spectra_ref, ids_ref, out_ref, alive_ref
+):
     count, slots, degrees = spectra_ref.shape
     levels = count // (2 * fields)
-    degree = rank_ref[0] * degrees + lax.broadcasted_iota(jnp.int32, (degrees, slots), 0)
-    alive = degree >= ids_ref[...]
+    ids = jnp.zeros((1, slots), jnp.int32)
+    for w, (first, last) in enumerate(pieces(ids_ref.shape[1], slots)):
+        ids = jnp.where(wave_ref[0] == w, ids_ref[:, first:last], ids)
+    degree = lat_ref[0] * degrees + lax.broadcasted_iota(jnp.int32, (degrees, slots), 0)
+    alive_ref[...] = jnp.where(degree >= ids, 1.0, 0.0)
+    alive = alive_ref[...]
     for i in range(count):
         field, level, part = i // (2 * levels), (i // 2) % levels, i % 2
-        turned = jnp.where(alive, spectra_ref[i].astype(F32).T, 0.0)
+        turned = spectra_ref[i].astype(F32).T * alive
         place = (level * fields + field) * 2 + part
         out_ref[place] = jnp.concatenate([turned] * repeats, axis=1)
 
@@ -129,13 +140,6 @@
     return [jnp.concatenate(tile, axis=1) for tile in tiles]
 
 
-def early_forward_kernel(spectra_ref, *refs):
-    *legendre_refs, out_ref = refs
-    for first, last in pieces(len(legendre_refs), 2):
-        for k, value in enumerate(forward_sums(legendre_refs[first:last], spectra_ref)):
-            out_ref[first + k] = value
-
-
 def put_row_messages(levels, owned, slots, out_ref, a, value):
     per_level = value.shape[0] // levels
     rows = value.shape[1] // slots * levels
@@ -147,17 +151,25 @@
         put_message(out_ref, (a * (rows // owned) + row // owned, row % owned), message)
 
 
+def early_forward_kernel(levels, owned, slots, spectra_ref, *refs):
+    *legendre_refs, out_ref = refs
+    for first, last in pieces(len(legendre_refs), 2):
+        for k, value in enumerate(forward_sums(legendre_refs[first:last], spectra_ref)):
+            put_row_messages(levels, owned, slots, out_ref, first + k, value)
+
+
 def last_forward_kernel(levels, owned, slots, groups, rank_ref, spectra_ref, *refs):
     *early_refs, out_ref = refs[: len(groups) - 1] + refs[-1:]
     legendre_refs = refs[len(groups) - 1 : -1]
-    put = functools.partial(put_row_messages, levels, owned, slots, out_ref)
     for places, ref in zip(groups[:-1], early_refs):
+        targets = ref.shape[0] // len(places)
         for k, d in enumerate(places):
-            put(rank_ref[0] ^ d, ref[k])
+            start = (rank_ref[0] ^ d) * targets
+            out_ref[pl.ds(start, targets)] = ref[k * targets : (k + 1) * targets]
     for first, last in pieces(len(legendre_refs), 2):
         values = forward_sums(legendre_refs[first:last], spectra_ref)
         for d, value in zip(groups[-1][first:last], values):
-            put(rank_ref[0] ^ d, value)
+            put_row_messages(levels, owned, slots, out_ref, rank_ref[0] ^ d, value)
 
 
 def loop_forward_kernel(levels, owned, slots, spectra_ref, legendre_ref, out_ref):
@@ -202,9 +214,20 @@
 
 
 def table_kernel(
-    levels, rank_ref, nlon_ref, coriolis_ref, weight_ref, ids_ref,
-    table_ref, left_ref, right_ref, share_ref, rotation_ref, base_ref, step_ref,
+    levels, rank_ref, ids_ref, nlon_far, coriolis_far, weight_far,
+    table_ref, left_ref, right_ref, share_ref, rotation_ref,
+    base_ref, step_ref, nlon_ref, coriolis_ref, weight_ref, sems,
 ):
+    copies = [
+        pltpu.make_async_copy(far, near, sems.at[i])
+        for i, (far, near) in enumerate(
+            [(nlon_far, nlon_ref), (coriolis_far, coriolis_ref), (weight_far, weight_ref)]
+        )
+    ]
+    for copy in copies:
+        copy.start()
+    for copy in copies:
+        copy.wait()
     owned = table_ref.shape[0]
     steps = step_ref.shape[1]
     waves = ids_ref.shape[1]
@@ -314,7 +337,7 @@
                     put(a, 0)
 
 
-def backward_kernel(levels, rank_ref, back_ref, ids_ref, *refs):
+def backward_kernel(levels, rank_ref, back_ref, alive_ref, *refs):
     *legendre_refs, out_ref, wide_ref, sums_ref, done_ref, sems = refs
     sources, _, _, columns = wide_ref.shape
     degrees = sums_ref.shape[1]
@@ -341,8 +364,7 @@
     else:
         lax.fori_loop(0, sources, lambda a, carry: spread(a, a) or carry, 0)
 
-    degree = rank_ref[0] * degrees + lax.broadcasted_iota(jnp.int32, (degrees, slots), 0)
-    alive = degree >= ids_ref[...]
+    alive = alive_ref[...]
     copies = []
     for own in pieces(outs, outs):
         for first, last in pieces(degrees, 16):
@@ -378,7 +400,7 @@
             folded = value[:, :slots]
             for lat in range(1, lats):
                 folded = folded + value[:, lat * slots : (lat + 1) * slots]
-            done_ref[i] = jnp.where(alive, folded, 0.0).T
+            done_ref[i] = (folded * alive).T
             copies.append(pltpu.make_async_copy(done_ref.at[i], out_ref.at[i], sems.at[i]))
             copies[-1].start()
     for copy in copies:
@@ -421,15 +443,18 @@
         blocks = lax.all_to_all(blocks.reshape(n_lat, degrees, columns), "lat", 0, 0, tiled=True)
         turned = {0: blocks}
 
-    own_ids = lax.dynamic_slice_in_dim(wave_m, wave_rank[0] * slots, slots, 0).reshape(1, slots)
     all_ids = wave_m.reshape(1, waves)
-    spectra_turned = call(
+    spectra_turned, alive = call(
         functools.partial(turn_spectra_kernel, lats, fields),
-        jax.ShapeDtypeStruct((2 * fields * levels, degrees, columns), F32),
-        [SMEM, VMEM, VMEM],
-        flops=10 * fields * levels * degrees * columns,
+        (
+            jax.ShapeDtypeStruct((2 * fields * levels, degrees, columns), F32),
+            jax.ShapeDtypeStruct((degrees, slots), F32),
+        ),
+        [SMEM, SMEM, VMEM, VMEM],
+        out_specs=(VMEM, VMEM),
+        flops=WORK * 10 * fields * levels * degrees * columns,
         bytes_accessed=8 * fields * levels * degrees * columns,
-    )(lat_rank, spectra.reshape(2 * fields * levels, slots, degrees), own_ids)
+    )(lat_rank, wave_rank, spectra.reshape(2 * fields * levels, slots, degrees), all_ids)
 
     row = call(
         functools.partial(table_kernel, levels),
@@ -440,29 +465,36 @@
             jax.ShapeDtypeStruct((owned, 8, places), F32),
             jax.ShapeDtypeStruct((owned, 8, places), F32),
         ),
-        [SMEM, SMEM, SMEM, SMEM, VMEM],
-        [pltpu.VMEM((2, BASE, waves), F32), pltpu.VMEM((2, steps, waves), F32)],
+        [SMEM, VMEM, HBM, HBM, HBM],
+        [
+            pltpu.VMEM((2, BASE, waves), F32),
+            pltpu.VMEM((2, steps, waves), F32),
+            pltpu.SMEM((lats,), jnp.int32),
+            pltpu.SMEM((lats,), F32),
+            pltpu.SMEM((lats,), F32),
+            pltpu.SemaphoreType.DMA((3,)),
+        ],
         out_specs=(VMEM,) * 5,
-        flops=16 * owned * places * waves,
+        flops=WORK * 16 * owned * places * waves,
         bytes_accessed=4 * owned * places * waves,
-    )(wave_rank, nlon, coriolis, gauss_quadrature_weight, all_ids)
+    )(wave_rank, all_ids, *[far(x) for x in (nlon, coriolis, gauss_quadrature_weight)])
     spectra_turned, *row = lax.optimization_barrier((spectra_turned, *row))
 
     message = jax.ShapeDtypeStruct(
         (n_lat * n_wave, owned) + message_shape(2 * fields, slots), BF16
     )
-    cost = 4 * fields * levels * degrees * columns
+    cost = WORK * 4 * fields * levels * degrees * columns
     if apart:
         groups = GROUPS[n_lat]
         early = []
         for part in groups[:-1]:
             early.append(
                 call(
-                    early_forward_kernel,
-                    jax.ShapeDtypeStruct((len(part), 2 * fields * levels, columns), F32),
+                    functools.partial(early_forward_kernel, levels, owned, slots),
+                    jax.ShapeDtypeStruct((len(part) * n_wave,) + message.shape[1:], BF16),
                     [VMEM] * (1 + len(part)),
                     flops=len(part) * cost,
-                    bytes_accessed=cost,
+                    bytes_accessed=cost // WORK,
                 )(spectra_turned, *[turned[d] for d in part])
             )
         partial = call(
@@ -470,7 +502,7 @@
             message,
             [SMEM] + [VMEM] * (len(groups) + len(groups[-1])),
             flops=len(groups[-1]) * cost,
-            bytes_accessed=cost,
+            bytes_accessed=cost // WORK,
         )(lat_rank, spectra_turned, *early, *[turned[d] for d in groups[-1]])
     else:
         partial = call(
@@ -478,7 +510,7 @@
             message,
             [VMEM, VMEM],
             flops=n_lat * cost,
-            bytes_accessed=cost,
+            bytes_accessed=cost // WORK,
         )(spectra_turned, turned[0])
     partial = lax.all_to_all(partial, ("lat", "wave"), 0, 0, tiled=True)
 
@@ -506,7 +538,7 @@
         out_specs=HBM,
         flops=2 * n_lat * outs * degrees * columns,
         bytes_accessed=8 * outs * degrees * slots,
-    )(lat_rank, back, own_ids, *[turned[d] for d in sorted(turned)])
+    )(lat_rank, back, alive, *[turned[d] for d in sorted(turned)])
     return out.reshape(2, levels, 2, slots, degrees)
 
 

time: 44.2 us -> 47.9 us (1.084)
  waiting for transfers between devices: 2.04 us -> 10.3 us
  starting transfers between devices: 12 us -> 8.38 us
  local copies, waits for them, and re-layouts: 3.63 us -> 1.76 us
  Pallas kernels: 6 us -> 6.86 us
    ppermute x7, waiting for transfers between devices: 2.04 us -> 10.3 us  [local(): lax.ppermute(blocks[d], 'lat', [(i, i ^ d) for i in range(n_lat)])]
    ppermute x7, starting transfers between devices: 12 us -> 8.38 us  [local(): lax.ppermute(blocks[d], 'lat', [(i, i ^ d) for i in range(n_lat)])]
    unnamed x10 -> x4, local copies, waits for them, and re-layouts: 2.18 us -> 1.07 us
    pallas_call x3 -> x4, Pallas kernels: 1.33 us -> 2.28 us  [the longest x3 1.43 us: local(): call(functools.partial(early_forward_kernel, levels, owned, slots), jax.S...]
    dynamic_slice x1 -> x0, local copies, waits for them, and re-layouts: 0.76 us -> none  [local(): lax.dynamic_slice_in_dim(wave_m, wave_rank[0] * slots, slots, 0)]
  transfers between devices with their start and end apart: 7 -> 7, of which waited for: 2 -> 3; matrix products, arithmetic and copies ran while one was open for 3% -> 1% of each run, Pallas kernels for 6% -> 8%
where the time goes in v1:
time: 47.9 us; the launch traced here: 47.7 us
  blocking collectives  20.4 us (43%)
  waiting for transfers between devices  10.3 us (22%)
  starting transfers between devices  8.38 us (17%)
  Pallas kernels  6.86 us (14%)
  local copies, waits for them, and re-layouts  1.76 us (4%)
    all_to_all x1, blocking collectives, local(): partial = lax.all_to_all(partial, ('lat', 'wave'), 0, 0, tiled=True)  11.2 us
    ppermute x7, waiting for transfers between devices, local(): lax.ppermute(blocks[d], 'lat', [(i, i ^ d) for i in range(n_lat)])  10.3 us
    all_to_all x1, blocking collectives, local(): back = lax.all_to_all(back, ('lat', 'wave'), 0, 0, tiled=True)  9.18 us
    ppermute x7, starting transfers between devices, local(): lax.ppermute(blocks[d], 'lat', [(i, i ^ d) for i in range(n_lat)])  8.38 us
    pallas_call x1, Pallas kernels, local(): call(functools.partial(backward_kernel, levels), jax.ShapeDtypeStruct((ou...  1.7 us
    pallas_call x3, Pallas kernels, local(): call(functools.partial(early_forward_kernel, levels, owned, slots), jax.S...  1.43 us
    pallas_call x1, Pallas kernels, local(): call(functools.partial(table_kernel, levels), (jax.ShapeDtypeStruct((owne...  1.34 us
    unnamed x4, local copies, waits for them, and re-layouts  1.07 us
  transfers between devices with their start and end apart: 7, of which 3 were waited for; matrix products, arithmetic and copies ran while one was open for 1% of the time, Pallas kernels for 8%

profile of v1, /device:TPU:0, one launch (start us, length us, event | category | flops | bytes accessed | tf_op | source)
XLA Modules:
  0.0 47.7 jit_solution(7470977827621772768)
XLA Ops:
  0.0 0.0 copy-start
  0.0 1.1 %copy-done = bf16[2,192,768]{2,1,0:T(8,128)(2,1)S(1)} copy-done((bf16[2,192,768]{2,1,0:T(8,128)(2,1)S(1)}, bf16[2,192,768]{2,1,0:T(8,128)(2,1)}, u32[]{:S(2)}) %copy-start) | copy-done | bytes 589848
  1.1 0.0 copy-start.1
  1.1 0.3 shard_map.66
  1.3 5.1 %collective-permute-start.3 = (bf16[96,384]{1,0:T(8,128)(2,1)S(1)}, bf16[96,384]{1,0:T(8,128)(2,1)S(1)}, u32[]{:S(2)}, u32[]{:S(2)}) collective-permute-start(bf16[96,384]{1,0:T(8,128)(2,1)S(1)} %get-tuple-element.37), channel_id=1, source_target_pairs={{0,24},{4,28},{8,16},{12,20},{16,8},{20,12},{24,0},{28,4},{1,25},{... | collective-permute-start | bytes 221192 | tf_op jit(solution)/shard_map/ppermute | solution.py:435
  6.5 0.0 collective-permute-start
  6.5 0.0 collective-permute-start.1
  6.5 1.9 %collective-permute-start.2 = (bf16[96,384]{1,0:T(8,128)(2,1)S(1)}, bf16[96,384]{1,0:T(8,128)(2,1)S(1)}, u32[]{:S(2)}, u32[]{:S(2)}) collective-permute-start(bf16[96,384]{1,0:T(8,128)(2,1)S(1)} %get-tuple-element.36), channel_id=1, source_target_pairs={{0,12},{4,8},{8,4},{12,0},{16,28},{20,24},{24,20},{28,16},{1,13},{... | collective-permute-start | bytes 221192 | tf_op jit(solution)/shard_map/ppermute | solution.py:435
  8.3 0.0 collective-permute-start.4
  8.4 0.7 %reshape.21.ids_ref = s32[1,768]{1,0:T(1,128)S(1)} reshape(s32[768]{0:T(1024)} %param.8) | data formatting | bytes 6144 | tf_op jit(solution)/shard_map/reshape | solution.py:446
  9.1 0.1 collective-permute-done.3.refs_0_.refs_6_
  9.2 1.3 %collective-permute-start.5 = (bf16[96,384]{1,0:T(8,128)(2,1)S(1)}, bf16[96,384]{1,0:T(8,128)(2,1)S(1)}, u32[]{:S(2)}, u32[]{:S(2)}) collective-permute-start(bf16[96,384]{1,0:T(8,128)(2,1)S(1)} %get-tuple-element.39), channel_id=1, source_target_pairs={{0,16},{4,20},{8,24},{12,28},{16,0},{20,4},{24,8},{28,12},{1,17},{... | collective-permute-start | bytes 221192 | tf_op jit(solution)/shard_map/ppermute | solution.py:435
  10.5 1.3 %shard_map.65 = (bf16[1,400,1536]{2,1,0:T(8,128)(2,1)S(1)}, f32[1,4,8,768]{3,2,1,0:T(8,128)S(1)}, f32[1,4,8,768]{3,2,1,0:T(8,128)S(1)}, f32[1,8,400]{2,1,0:T(8,128)S(1)}, f32[1,8,400]{2,1,0:T(8,128)S(1)}) custom-call(s32[1]{0:T(128)} %bitcast.1.wave_ref.rank_ref, s32[1,768]{1,0:T(1,128)S(1)} %reshape.21.ids_ref, s32[2]{0:T(128)} %nlon_far.1, f32[2]{0:T(128)} %coriolis_far.1, ...), custom_call_target="tpu_custom_call" | custom-call | flops 629145600 | bytes 1228800 | tf_op jit(solution)/shard_map/pallas_call | solution.py:459
  11.8 0.0 copy-done.1
  11.9 0.8 %shard_map.64 = (f32[12,96,384]{2,1,0:T(8,128)S(1)}, f32[96,192]{1,0:T(8,128)S(1)}) custom-call(s32[1]{0:T(128)} %bitcast.lat_ref.rank_ref, s32[1]{0:T(128)} %bitcast.1.wave_ref.rank_ref, bf16[12,192,96]{2,1,0:T(8,128)(2,1)S(1)} %bitcast.6, s32[1,768]{1,0:T(1,128)S(1)} %reshape.21.ids_ref), custom_call_target="tpu_custom_call" | custom-call | flops 283115520 | bytes 1769472 | tf_op jit(solution)/shard_map/pallas_call | solution.py:447
  12.7 4.8 %collective-permute-done.5.refs_0_.refs_4_ = bf16[96,384]{1,0:T(8,128)(2,1)S(1)} collective-permute-done((bf16[96,384]{1,0:T(8,128)(2,1)S(1)}, bf16[96,384]{1,0:T(8,128)(2,1)S(1)}, u32[]{:S(2)}, u32[]{:S(2)}) %collective-permute-start.5) | collective-permute-done | bytes 73760 | tf_op jit(solution)/shard_map/ppermute | solution.py:435
  17.5 0.0 collective-permute-start.6
  17.6 0.3 shard_map.69.refs_2_
  17.9 0.0 collective-permute-done.4.refs_1_.refs_7_
  17.9 0.4 shard_map.68.refs_1_
  18.2 0.0 collective-permute-done.refs_1_
  18.3 0.0 collective-permute-done.1.refs_2_
  18.3 0.0 collective-permute-done.2.refs_3_
  18.3 0.8 %shard_map.67.refs_0_ = bf16[16,1,5,2,128]{4,3,2,1,0:T(2,128)(2,1)S(1)} custom-call(f32[12,96,384]{2,1,0:T(8,128)S(1)} %get-tuple-element.32.spectra_ref, bf16[96,384]{1,0:T(8,128)(2,1)S(1)} %get-tuple-element.33.refs_0_, bf16[96,384]{1,0:T(8,128)(2,1)S(1)} %collective-permute-done.refs_1_, bf16[96,384]{1,0:T(8,128)(2,1)S(1)} %collective-permute-done.1.refs_2_, ...), custom_call_target="tpu_custom_call" | custom-call | flops 452984832 | bytes 884736 | tf_op jit(solution)/shard_map/pallas_call | solution.py:492
  19.0 5.3 %collective-permute-done.6.refs_3_.refs_5_ = bf16[96,384]{1,0:T(8,128)(2,1)S(1)} collective-permute-done((bf16[96,384]{1,0:T(8,128)(2,1)S(1)}, bf16[96,384]{1,0:T(8,128)(2,1)S(1)}, u32[]{:S(2)}, u32[]{:S(2)}) %collective-permute-start.6) | collective-permute-done | bytes 73760 | tf_op jit(solution)/shard_map/ppermute | solution.py:435
  24.4 0.3 shard_map.70
  24.7 11.2 %all_to_all.10.partial_ref = bf16[32,1,5,2,128]{4,3,2,1,0:T(2,128)(2,1)S(1)} all-to-all(bf16[32,1,5,2,128]{4,3,2,1,0:T(2,128)(2,1)S(1)} %shard_map.70), channel_id=1, replica_groups=mesh['lat'=8,'wave'=4] {'lat','wave'}, dimensions={0} | all-to-all | bytes 163840 | tf_op jit(solution)/shard_map/all_to_all | solution.py:515
  35.8 1.0 %shard_map.71 = bf16[32,1,4,192]{3,2,1,0:T(4,128)(2,1)S(1)} custom-call(bf16[32,1,5,2,128]{4,3,2,1,0:T(2,128)(2,1)S(1)} %all_to_all.10.partial_ref, bf16[1,400,1536]{2,1,0:T(8,128)(2,1)S(1)} %get-tuple-element.41.table_ref, f32[1,4,8,768]{3,2,1,0:T(8,128)S(1)} %get-tuple-element.42.left_ref, f32[1,4,8,768]{3,2,1,0:T(8,128)S(1)} %get-tuple-element.43.right_ref, ...), custom_call_target="tpu_custom_call" | custom-call | flops 39321600 | bytes 1228800 | tf_op jit(solution)/shard_map/pallas_call | solution.py:517
  36.8 9.2 %all_to_all.11.back_ref = bf16[32,1,4,192]{3,2,1,0:T(4,128)(2,1)S(1)} all-to-all(bf16[32,1,4,192]{3,2,1,0:T(4,128)(2,1)S(1)} %shard_map.71), channel_id=1, replica_groups=mesh['lat'=8,'wave'=4] {'lat','wave'}, dimensions={0} | all-to-all | bytes 98304 | tf_op jit(solution)/shard_map/all_to_all | solution.py:525
  46.0 1.7 %shard_map.72 = f32[8,192,96]{2,1,0:T(8,128)} custom-call(s32[1]{0:T(128)} %bitcast.lat_ref.rank_ref, bf16[32,1,4,192]{3,2,1,0:T(4,128)(2,1)S(1)} %all_to_all.11.back_ref, f32[96,192]{1,0:T(8,128)S(1)} %get-tuple-element.46.alive_ref, bf16[96,384]{1,0:T(8,128)(2,1)S(1)} %get-tuple-element.33.refs_0_, bf16[96,384]{1,0:T(8,128)(2,1)S(1)} %collective-permute-done.refs_1_, ...), custom_call_target="tpu_custom_call" | custom-call | flops 4718592 | bytes 1179648 | tf_op jit(solution)/shard_map/pallas_call | solution.py:528
Async XLA Ops:
  0.0 1.1 %copy-start = (bf16[2,192,768]{2,1,0:T(8,128)(2,1)S(1)}, bf16[2,192,768]{2,1,0:T(8,128)(2,1)}, u32[]{:S(2)}) copy-start(bf16[2,192,768]{2,1,0:T(8,128)(2,1)} %param.7) | copy-start | bytes 1769476
  1.1 10.8 %copy-start.1 = (bf16[3,2,2,192,96]{4,3,2,1,0:T(8,128)(2,1)S(1)}, bf16[3,2,2,192,96]{4,3,2,1,0:T(8,128)(2,1)}, u32[]{:S(2)}) copy-start(bf16[3,2,2,192,96]{4,3,2,1,0:T(8,128)(2,1)} %param.6) | copy-start | bytes 1327108
  1.3 7.8 %collective-permute-start.3 = (bf16[96,384]{1,0:T(8,128)(2,1)S(1)}, bf16[96,384]{1,0:T(8,128)(2,1)S(1)}, u32[]{:S(2)}, u32[]{:S(2)}) collective-permute-start(bf16[96,384]{1,0:T(8,128)(2,1)S(1)} %get-tuple-element.37), channel_id=1, source_target_pairs={{0,24},{4,28},{8,16},{12,20},{16,8},{20,12},{24,0},{28,4},{1,25},{... | collective-permute-start | bytes 221192 | tf_op jit(solution)/shard_map/ppermute | solution.py:435
  6.5 11.8 %collective-permute-start = (bf16[96,384]{1,0:T(8,128)(2,1)S(1)}, bf16[96,384]{1,0:T(8,128)(2,1)S(1)}, u32[]{:S(2)}, u32[]{:S(2)}) collective-permute-start(bf16[96,384]{1,0:T(8,128)(2,1)S(1)} %get-tuple-element.34), channel_id=1, source_target_pairs={{0,4},{4,0},{8,12},{12,8},{16,20},{20,16},{24,28},{28,24},{1,5},{5... | collective-permute-start | bytes 221192 | tf_op jit(solution)/shard_map/ppermute | solution.py:435
  6.5 11.8 %collective-permute-start.1 = (bf16[96,384]{1,0:T(8,128)(2,1)S(1)}, bf16[96,384]{1,0:T(8,128)(2,1)S(1)}, u32[]{:S(2)}, u32[]{:S(2)}) collective-permute-start(bf16[96,384]{1,0:T(8,128)(2,1)S(1)} %get-tuple-element.35), channel_id=1, source_target_pairs={{0,8},{4,12},{8,0},{12,4},{16,24},{20,28},{24,16},{28,20},{1,9},{5... | collective-permute-start | bytes 221192 | tf_op jit(solution)/shard_map/ppermute | solution.py:435
  6.5 11.8 %collective-permute-start.2 = (bf16[96,384]{1,0:T(8,128)(2,1)S(1)}, bf16[96,384]{1,0:T(8,128)(2,1)S(1)}, u32[]{:S(2)}, u32[]{:S(2)}) collective-permute-start(bf16[96,384]{1,0:T(8,128)(2,1)S(1)} %get-tuple-element.36), channel_id=1, source_target_pairs={{0,12},{4,8},{8,4},{12,0},{16,28},{20,24},{24,20},{28,16},{1,13},{... | collective-permute-start | bytes 221192 | tf_op jit(solution)/shard_map/ppermute | solution.py:435
  8.3 9.5 %collective-permute-start.4 = (bf16[96,384]{1,0:T(8,128)(2,1)S(1)}, bf16[96,384]{1,0:T(8,128)(2,1)S(1)}, u32[]{:S(2)}, u32[]{:S(2)}) collective-permute-start(bf16[96,384]{1,0:T(8,128)(2,1)S(1)} %get-tuple-element.38), channel_id=1, source_target_pairs={{0,28},{4,24},{8,20},{12,16},{16,12},{20,8},{24,4},{28,0},{1,29},{... | collective-permute-start | bytes 221192 | tf_op jit(solution)/shard_map/ppermute | solution.py:435
  9.2 8.4 %collective-permute-start.5 = (bf16[96,384]{1,0:T(8,128)(2,1)S(1)}, bf16[96,384]{1,0:T(8,128)(2,1)S(1)}, u32[]{:S(2)}, u32[]{:S(2)}) collective-permute-start(bf16[96,384]{1,0:T(8,128)(2,1)S(1)} %get-tuple-element.39), channel_id=1, source_target_pairs={{0,16},{4,20},{8,24},{12,28},{16,0},{20,4},{24,8},{28,12},{1,17},{... | collective-permute-start | bytes 221192 | tf_op jit(solution)/shard_map/ppermute | solution.py:435
  17.5 6.8 %collective-permute-start.6 = (bf16[96,384]{1,0:T(8,128)(2,1)S(1)}, bf16[96,384]{1,0:T(8,128)(2,1)S(1)}, u32[]{:S(2)}, u32[]{:S(2)}) collective-permute-start(bf16[96,384]{1,0:T(8,128)(2,1)S(1)} %get-tuple-element.40), channel_id=1, source_target_pairs={{0,20},{4,16},{8,28},{12,24},{16,4},{20,0},{24,12},{28,8},{1,21},{... | collective-permute-start | bytes 221192 | tf_op jit(solution)/shard_map/ppermute | solution.py:435
